TPU v7x, 32 devices: a whole 2x2x4 slice. The times are simulated.
32 devices in a mesh: tensor: 4 (over y, x), seq: 8 (over z, core).
Axes of the slice: x: 2, y: 2, z: 4, core: 2. Of those that a mesh axis runs over, the one named last changes fastest.
Arguments:
- key_states: bfloat16 [8, 2, 4096, 1024], P(None, None, 'seq', 'tensor'), may hold values from -6 to 6
- value_states: bfloat16 [8, 2, 4096, 1024], P(None, None, 'seq', 'tensor'), may hold values from -6 to 6
- bin_index: int32 [8, 8, 4096], P(None, 'tensor', 'seq'), may hold values from 0 to 4095
- retain_count: int32 [8], replicated, may hold values from 1 to 4096
Outputs:
- histogram: float32 [8, 8, 2, 4096], P(None, 'tensor', None, 'seq')
- threshold: int32 [8], replicated
All inputs are finite; a program needn't handle non-finite values.
Results may differ from a plain program's by a relative error of at most 0.0029.
Values sent between devices are 32-bit elements; how exact they have to be, the bound alone decides.
No kernel may reach another device: no remote copies, remote signals or barrier semaphores. Data moves between devices by JAX's collectives and lax.ppermute only.
A program may use at most 64 MiB of HBM per device.

v0:
```python
import functools

import jax
import jax.numpy as jnp
from jax import lax
from jax.experimental import pallas as pl
from jax.experimental.pallas import tpu as pltpu
from jax.sharding import PartitionSpec as P


HD = 128
BINS = 4096
LANES = 128
VMEM = pltpu.MemorySpace.VMEM
SMEM = pltpu.MemorySpace.SMEM
NT = (((1,), (1,)), ((), ()))
MIB = 1 << 20


def lane_onehot(row, lanes):
    return (lax.broadcasted_iota(jnp.int32, (lanes, row.shape[1]), 0) == (row & (lanes - 1))).astype(jnp.bfloat16)


def cosine(ref, p, h):
    first = ref[p, 0, :, h * HD : (h + 1) * HD].T.astype(jnp.float32)
    second = ref[p, 1, :, h * HD : (h + 1) * HD].T.astype(jnp.float32)
    inner = jnp.sum(first * second, axis=0, keepdims=True)
    first_sq = jnp.sum(first * first, axis=0, keepdims=True)
    second_sq = jnp.sum(second * second, axis=0, keepdims=True)
    return inner * lax.rsqrt((first_sq + 1.0) * (second_sq + 1.0))


def parity(x, size):
    odd = x
    for k in range(1, (size - 1).bit_length()):
        odd = odd ^ (x >> k)
    return odd & 1


def side_of_bins():
    return (lax.axis_index("seq") & 1) ^ parity(lax.axis_index("tensor"), lax.axis_size("tensor"))


def add_counts(bins, keep_ref, give_ref):
    pairs, heads, tokens = bins.shape
    blocks = BINS // LANES
    rows = lax.broadcasted_iota(jnp.int32, (blocks, tokens), 0)
    high = rows ^ (side_of_bins() * (blocks // 2))
    for p in range(pairs):
        total = None
        for h in range(heads):
            row = bins[p, h : h + 1, :]
            left = (high == (row // LANES)).astype(jnp.bfloat16)
            part = lax.dot_general(left, lane_onehot(row, LANES), NT, preferred_element_type=jnp.float32)
            total = part if total is None else total + part
        keep_ref[p] = total[: blocks // 2]
        give_ref[p] = total[blocks // 2 :]


def add_tables(ranges, bins, work, keys, values, keep_ref, give_ref):
    _, heads, tokens = bins.shape
    lanes = keep_ref.shape[-1]
    per = BINS // lanes // ranges
    rows = ranges * 2 * per
    index = lax.broadcasted_iota(jnp.int32, (rows, tokens), 0)
    block = index // (2 * per)
    half = ranges // 2
    away = (block >= half).astype(jnp.int32)
    block = block - half * away
    block = 2 * block + away
    high = (block ^ lax.axis_index("seq")) * per + index % per
    is_key = (index // per) % 2 == 0
    for p in work:
        for h in range(heads):
            row = bins[p, h : h + 1, :]
            weight = jnp.where(is_key, cosine(keys, p, h), cosine(values, p, h))
            left = jnp.where(high == (row // lanes), weight, 0.0).astype(jnp.bfloat16)
            table = lax.dot_general(left, lane_onehot(row, lanes), NT, preferred_element_type=jnp.float32)
            table = table.reshape(ranges, 2 * per, lanes)
            keep_ref[:, p, h] = table[:half]
            give_ref[:, p, h] = table[half:]


def count_kernel(bin_ref, target_ref, keep_ref, give_ref, bins, goal_ref, target, sem, target_sem):
    copy = pltpu.make_async_copy(bin_ref, bins, sem)
    target_copy = pltpu.make_async_copy(target_ref, target, target_sem)
    copy.start()
    target_copy.start()
    copy.wait()
    add_counts(bins, keep_ref, give_ref)
    target_copy.wait()
    goal_ref[...] = jnp.concatenate([jnp.full((1, LANES), target[p].astype(jnp.float32)) for p in range(goal_ref.shape[0])], axis=0)


def hist_kernel(ranges, work, key_ref, value_ref, bins, *refs):
    add_tables(ranges, bins, work, key_ref, value_ref, *refs[-2:])


def threshold_kernel(everything, goal_ref, own_ref, out_ref):
    pairs, blocks, lanes = own_ref.shape
    counts = own_ref[...].reshape(pairs * blocks, lanes)
    column = lax.broadcasted_iota(jnp.int32, (lanes, 2 * lanes), 1)
    upper = ((lax.broadcasted_iota(jnp.int32, (lanes, 2 * lanes), 0) <= column) | (column >= lanes)).astype(jnp.bfloat16)
    sums, scale, rest = 0.0, 1.0, counts
    while scale <= everything:
        above = jnp.floor(rest * (1.0 / 256.0))
        digit = rest - above * 256.0
        sums = sums + scale * jnp.dot(digit.astype(jnp.bfloat16), upper, preferred_element_type=jnp.float32)
        scale, rest = scale * 256.0, above
    within = sums[:, :lanes].reshape(pairs, blocks, lanes)
    total = sums[:, lanes:].reshape(pairs, blocks, lanes)
    line = lax.broadcasted_iota(jnp.int32, (blocks, lanes), 0)
    slot = lax.broadcasted_iota(jnp.int32, (pairs, lanes), 0)
    top_half = side_of_bins() == 1
    running = jnp.zeros((blocks, lanes), jnp.float32)
    found = jnp.zeros((pairs, lanes), jnp.float32)
    for p in range(pairs):
        upto = total[p]
        step = 1
        while step < blocks:
            upto = upto + jnp.where(line >= step, pltpu.roll(upto, step, 0), 0.0)
            step *= 2
        below_half = jnp.where(top_half, everything - upto[blocks - 1 :], 0.0)
        running = running + within[p] + (upto - total[p]) + below_half
        below = (running < goal_ref[p : p + 1, :]).astype(jnp.float32)
        found = jnp.where(slot == p, jnp.sum(below, axis=0, keepdims=True), found)
    out_ref[...] = found


def final_kernel(own_ref, other_ref, *refs):
    *parts, out_ref, threshold_ref = refs
    pairs, heads, rows, lanes = parts[-1].shape
    per = rows // 2
    for p in range(pairs):
        for h in range(heads):
            tile = parts[0][p, h]
            for part in parts[1:]:
                tile = tile + part[p, h]
            for r in range(2):
                for k in range(per):
                    out_ref[p, h, r : r + 1, k * lanes : (k + 1) * lanes] = tile[r * per + k : r * per + k + 1]
    found = (own_ref[...] + other_ref[...]).astype(jnp.bfloat16)
    ones = jnp.ones((8, found.shape[1]), jnp.bfloat16)
    threshold_ref[...] = lax.dot_general(ones, found, NT, preferred_element_type=jnp.float32)[0:1].astype(jnp.int32)


def per_device(key_states, value_states, bin_index, retain_count):
    pairs, heads, tokens = bin_index.shape
    ranges, columns = lax.axis_size("seq"), lax.axis_size("tensor")
    lanes = min(LANES, BINS // ranges)
    per = BINS // lanes // ranges
    bins = pltpu.with_memory_space_constraint(bin_index, pltpu.HBM)
    target = pltpu.with_memory_space_constraint(retain_count, pltpu.HBM)
    whole = pl.BlockSpec(memory_space=VMEM)
    scalar = pl.BlockSpec(memory_space=SMEM)

    def permute(x, tensor_bit, seq_bit):
        pairing = [(t * ranges + j, (t ^ tensor_bit) * ranges + (j ^ seq_bit)) for t in range(columns) for j in range(ranges)]
        return lax.ppermute(x, ("tensor", "seq"), pairing)

    apart = pl.BlockSpec(memory_space=pl.ANY)
    half = jax.ShapeDtypeStruct((pairs, BINS // LANES // 2, LANES), jnp.float32)
    side = jax.ShapeDtypeStruct((ranges // 2, pairs, heads, 2 * per, lanes), jnp.float32)
    mine, give, bins, goal = pl.pallas_call(
        count_kernel,
        out_shape=(half, half, jax.ShapeDtypeStruct(bin_index.shape, jnp.int32), jax.ShapeDtypeStruct((pairs, LANES), jnp.float32)),
        in_specs=[apart] * 2,
        out_specs=(whole,) * 4,
        scratch_shapes=[pltpu.SMEM((pairs,), jnp.int32), pltpu.SemaphoreType.DMA, pltpu.SemaphoreType.DMA],
        cost_estimate=pl.CostEstimate(flops=10000000000, bytes_accessed=100000000, transcendentals=0),
        compiler_params=pltpu.CompilerParams(vmem_limit_bytes=4 * MIB),
        name="counts",
    )(bins, target)
    sides = ()
    for piece in range(2):
        sides = pl.pallas_call(
            functools.partial(hist_kernel, ranges, range(pairs)[SPLIT[piece]]),
            out_shape=(side, side),
            in_specs=[whole] * 3 + [apart] * len(sides),
            out_specs=(whole,) * 2,
            input_output_aliases={3: 0, 4: 1} if sides else {},
            compiler_params=pltpu.CompilerParams(vmem_limit_bytes=16 * MIB),
            name="hist",
        )(key_states, value_states, bins, *sides)
    keep, away = sides

    def plus(x, y):
        return x + y

    mine = plus(mine, permute(give, 0, 1))
    bit = 2
    while bit < ranges:
        mine = plus(mine, permute(mine, 0, bit))
        bit *= 2
    bit = 1
    while bit < columns:
        mine = plus(mine, permute(mine, bit, 1))
        bit *= 2
    everything = float(tokens * ranges * heads * lax.axis_size("tensor"))
    found = pl.pallas_call(
        functools.partial(threshold_kernel, everything),
        out_shape=jax.ShapeDtypeStruct((pairs, LANES), jnp.float32),
        in_specs=[whole] * 2,
        out_specs=whole,
        compiler_params=pltpu.CompilerParams(vmem_limit_bytes=6 * MIB),
        name="threshold",
    )(goal, mine)
    other = permute(found, 0, 1)

    got = permute(away, 0, 1)
    parts = [[keep[j], got[j]] for j in range(ranges // 2)]
    total = lambda terms: functools.reduce(jnp.add, terms)
    bit = 2
    while bit < ranges:
        kept = []
        for j in range(0, len(parts), 2):
            part = permute(total(parts[j + 1]), 0, bit)
            kept.append([*parts[j], part])
        parts = kept
        bit *= 2
    parts = parts[0]
    histogram, threshold = pl.pallas_call(
        final_kernel,
        out_shape=(
            jax.ShapeDtypeStruct((pairs, heads, 2, per * lanes), jnp.float32),
            jax.ShapeDtypeStruct((1, pairs), jnp.int32),
        ),
        in_specs=[whole] * (2 + len(parts)),
        out_specs=(whole, whole),
        compiler_params=pltpu.CompilerParams(vmem_limit_bytes=14 * MIB),
        name="final",
    )(found, other, *parts)
    return (histogram, threshold.reshape(pairs))


SPLIT = (slice(0, 5), slice(5, None))


def solution(mesh):
    in_specs = (
        P(None, None, "seq", "tensor"),
        P(None, None, "seq", "tensor"),
        P(None, "tensor", "seq"),
        P(),
    )
    out_specs = (P(None, "tensor", None, "seq"), P())
    return jax.shard_map(per_device, mesh=mesh, in_specs=in_specs, out_specs=out_specs, check_vma=False)
```

profile of v0, /device:TPU:0, one launch (start us, length us, event | category | flops | bytes accessed | tf_op | source)
XLA Modules:
  0.0 35.4 jit_solution(1343296129731858908)
XLA Ops:
  0.6 0.0 copy-start.1
  0.6 0.0 copy-start
  0.7 1.8 %counts.1 = (f32[8,16,128]{2,1,0:T(8,128)S(1)}, f32[8,16,128]{2,1,0:T(8,128)S(1)}, s32[8,2,512]{2,1,0:T(2,128)S(1)}, f32[8,128]{1,0:T(8,128)S(1)}) custom-call(s32[8,2,512]{2,1,0:T(2,128)} %bin_ref.1, s32[8]{0:T(128)} %target_ref.1), custom_call_target="tpu_custom_call" | custom-call | flops 10000000000 | bytes 100000000 | tf_op jit(solution)/shard_map/counts/pallas_call | solution.py:164
  2.4 0.4 %copy-done.1 = bf16[8,2,512,256]{3,2,1,0:T(8,128)(2,1)S(1)} copy-done((bf16[8,2,512,256]{3,2,1,0:T(8,128)(2,1)S(1)}, bf16[8,2,512,256]{3,2,1,0:T(8,128)(2,1)}, u32[]{:S(2)}) %copy-start.1) | copy-done | bytes 4194328
  2.8 1.3 %copy-done = bf16[8,2,512,256]{3,2,1,0:T(8,128)(2,1)S(1)} copy-done((bf16[8,2,512,256]{3,2,1,0:T(8,128)(2,1)S(1)}, bf16[8,2,512,256]{3,2,1,0:T(8,128)(2,1)}, u32[]{:S(2)}) %copy-start) | copy-done | bytes 4194328
  4.1 2.1 %hist.2 = (f32[4,8,2,8,128]{4,3,2,1,0:T(8,128)S(1)}, f32[4,8,2,8,128]{4,3,2,1,0:T(8,128)S(1)}) custom-call(bf16[8,2,512,256]{3,2,1,0:T(8,128)(2,1)S(1)} %copy-done, bf16[8,2,512,256]{3,2,1,0:T(8,128)(2,1)S(1)} %copy-done.1, s32[8,2,512]{2,1,0:T(2,128)S(1)} %get-tuple-element.15.bins), custom_call_target="tpu_custom_call" | custom-call | tf_op jit(solution)/shard_map/hist/pallas_call | solution.py:176
  6.2 1.4 %hist.3 = (f32[4,8,2,8,128]{4,3,2,1,0:T(8,128)S(1)}, f32[4,8,2,8,128]{4,3,2,1,0:T(8,128)S(1)}) custom-call(bf16[8,2,512,256]{3,2,1,0:T(8,128)(2,1)S(1)} %copy-done, bf16[8,2,512,256]{3,2,1,0:T(8,128)(2,1)S(1)} %copy-done.1, s32[8,2,512]{2,1,0:T(2,128)S(1)} %get-tuple-element.15.bins, ...), custom_call_target="tpu_custom_call", output_to_operand_aliasing={{0}: (3, {}), {1}: (4, {})} | custom-call | tf_op jit(solution)/shard_map/hist/pallas_call | solution.py:176
  7.6 0.6 %collective-permute-start.6 = (f32[4,8,2,8,128]{4,3,2,1,0:T(8,128)S(1)}, f32[4,8,2,8,128]{4,3,2,1,0:T(8,128)S(1)}, u32[]{:S(2)}, u32[]{:S(2)}) collective-permute-start(f32[4,8,2,8,128]{4,3,2,1,0:T(8,128)S(1)} %get-tuple-element.19), channel_id=1, source_target_pairs={{0,1},{1,0},{2,3},{3,2},{4,5},{5,4},{6,7},{7,6},{8,9},{9,8},{10,11... | collective-permute-start | bytes 786440 | tf_op jit(solution)/shard_map/ppermute | solution.py:159
  8.1 0.1 collective-permute-start
  8.2 1.2 %collective-permute-done = f32[8,16,128]{2,1,0:T(8,128)S(1)} collective-permute-done((f32[8,16,128]{2,1,0:T(8,128)S(1)}, f32[8,16,128]{2,1,0:T(8,128)S(1)}, u32[]{:S(2)}, u32[]{:S(2)}) %collective-permute-start) | collective-permute-done | bytes 65568 | tf_op jit(solution)/shard_map/ppermute | solution.py:159
  9.4 3.0 %collective-permute-start.1 = (f32[8,16,128]{2,1,0:T(8,128)S(1)}, f32[8,16,128]{2,1,0:T(8,128)S(1)}, u32[]{:S(2)}, u32[]{:S(2)}) collective-permute-start(f32[8,16,128]{2,1,0:T(8,128)S(1)} %add.36), channel_id=1, source_target_pairs={{0,2},{1,3},{2,0},{3,1},{4,6},{5,7},{6,4},{7,5},{8,10},{9,11},{10,... | collective-permute-start | bytes 196616 | tf_op jit(solution)/shard_map/ppermute | solution.py:159
  12.4 2.4 %collective-permute-done.1 = f32[8,16,128]{2,1,0:T(8,128)S(1)} collective-permute-done((f32[8,16,128]{2,1,0:T(8,128)S(1)}, f32[8,16,128]{2,1,0:T(8,128)S(1)}, u32[]{:S(2)}, u32[]{:S(2)}) %collective-permute-start.1) | collective-permute-done | bytes 65568 | tf_op jit(solution)/shard_map/ppermute | solution.py:159
  14.8 2.9 %collective-permute-start.2 = (f32[8,16,128]{2,1,0:T(8,128)S(1)}, f32[8,16,128]{2,1,0:T(8,128)S(1)}, u32[]{:S(2)}, u32[]{:S(2)}) collective-permute-start(f32[8,16,128]{2,1,0:T(8,128)S(1)} %add.37), channel_id=1, source_target_pairs={{0,4},{1,5},{2,6},{3,7},{4,0},{5,1},{6,2},{7,3},{8,12},{9,13},{10,... | collective-permute-start | bytes 196616 | tf_op jit(solution)/shard_map/ppermute | solution.py:159
  17.8 2.3 %collective-permute-done.2 = f32[8,16,128]{2,1,0:T(8,128)S(1)} collective-permute-done((f32[8,16,128]{2,1,0:T(8,128)S(1)}, f32[8,16,128]{2,1,0:T(8,128)S(1)}, u32[]{:S(2)}, u32[]{:S(2)}) %collective-permute-start.2) | collective-permute-done | bytes 65568 | tf_op jit(solution)/shard_map/ppermute | solution.py:159
  20.1 0.1 collective-permute-start.3
  20.2 0.0 collective-permute-done.6
  20.2 1.9 %collective-permute-start.8 = (f32[8,2,8,128]{3,2,1,0:T(8,128)S(1)}, f32[8,2,8,128]{3,2,1,0:T(8,128)S(1)}, u32[]{:S(2)}, u32[]{:S(2)}) collective-permute-start(f32[8,2,8,128]{3,2,1,0:T(8,128)S(1)} %get-tuple-element.22), channel_id=1, source_target_pairs={{0,2},{1,3},{2,0},{3,1},{4,6},{5,7},{6,4},{7,5},{8,10},{9,11},{10,... | collective-permute-start | bytes 196616 | tf_op jit(solution)/shard_map/ppermute | solution.py:159
  22.1 2.1 %collective-permute-done.3 = f32[8,16,128]{2,1,0:T(8,128)S(1)} collective-permute-done((f32[8,16,128]{2,1,0:T(8,128)S(1)}, f32[8,16,128]{2,1,0:T(8,128)S(1)}, u32[]{:S(2)}, u32[]{:S(2)}) %collective-permute-start.3) | collective-permute-done | bytes 65568 | tf_op jit(solution)/shard_map/ppermute | solution.py:159
  24.2 1.9 %collective-permute-start.4 = (f32[8,16,128]{2,1,0:T(8,128)S(1)}, f32[8,16,128]{2,1,0:T(8,128)S(1)}, u32[]{:S(2)}, u32[]{:S(2)}) collective-permute-start(f32[8,16,128]{2,1,0:T(8,128)S(1)} %add.39), channel_id=1, source_target_pairs={{0,17},{1,16},{2,19},{3,18},{4,21},{5,20},{6,23},{7,22},{8,25},{9,... | collective-permute-start | bytes 196616 | tf_op jit(solution)/shard_map/ppermute | solution.py:159
  26.1 1.6 %collective-permute-start.7 = (f32[8,2,8,128]{3,2,1,0:T(8,128)S(1)}, f32[8,2,8,128]{3,2,1,0:T(8,128)S(1)}, u32[]{:S(2)}, u32[]{:S(2)}) collective-permute-start(f32[8,2,8,128]{3,2,1,0:T(8,128)S(1)} %get-tuple-element.23), channel_id=1, source_target_pairs={{0,2},{1,3},{2,0},{3,1},{4,6},{5,7},{6,4},{7,5},{8,10},{9,11},{10,... | collective-permute-start | bytes 196616 | tf_op jit(solution)/shard_map/ppermute | solution.py:159
  27.7 0.0 collective-permute-done.8
  27.7 3.2 %collective-permute-start.9 = (f32[8,2,8,128]{3,2,1,0:T(8,128)S(1)}, f32[8,2,8,128]{3,2,1,0:T(8,128)S(1)}, u32[]{:S(2)}, u32[]{:S(2)}) collective-permute-start(f32[8,2,8,128]{3,2,1,0:T(8,128)S(1)} %fusion.2), channel_id=1, source_target_pairs={{0,4},{1,5},{2,6},{3,7},{4,0},{5,1},{6,2},{7,3},{8,12},{9,13},{10,... | collective-permute-start | bytes 196616 | tf_op jit(solution)/shard_map/ppermute | solution.py:159
  31.0 0.0 collective-permute-done.4
  31.0 0.2 threshold.1.own_ref
  31.2 0.1 collective-permute-start.5
  31.3 0.0 collective-permute-done.7.refs_2_
  31.3 1.1 %collective-permute-done.5.other_ref = f32[8,128]{1,0:T(8,128)S(1)} collective-permute-done((f32[8,128]{1,0:T(8,128)S(1)}, f32[8,128]{1,0:T(8,128)S(1)}, u32[]{:S(2)}, u32[]{:S(2)}) %collective-permute-start.5) | collective-permute-done | bytes 4128 | tf_op jit(solution)/shard_map/ppermute | solution.py:159
  32.4 2.3 %collective-permute-done.9.refs_3_ = f32[8,2,8,128]{3,2,1,0:T(8,128)S(1)} collective-permute-done((f32[8,2,8,128]{3,2,1,0:T(8,128)S(1)}, f32[8,2,8,128]{3,2,1,0:T(8,128)S(1)}, u32[]{:S(2)}, u32[]{:S(2)}) %collective-permute-start.9) | collective-permute-done | bytes 65568 | tf_op jit(solution)/shard_map/ppermute | solution.py:159
  34.7 0.7 %final.1 = (f32[8,2,2,512]{3,2,1,0:T(2,128)}, s32[1,8]{1,0:T(1,128)}) custom-call(f32[8,128]{1,0:T(8,128)S(1)} %threshold.1.own_ref, f32[8,128]{1,0:T(8,128)S(1)} %collective-permute-done.5.other_ref, f32[8,2,8,128]{3,2,1,0:T(8,128)S(1)} %get-tuple-element.24.refs_0_, f32[8,2,8,128]{3,2,1,0:T(8,128)S(1)} %get-tuple-element.25.refs_1_, ...), custom_call_target="tpu_custom_call" | custom-call | tf_op jit(solution)/shard_map/final/pallas_call | solution.py:222
  (7 shorter events, 0.1 us)
Async XLA Ops:
  0.6 2.2 %copy-start.1 = (bf16[8,2,512,256]{3,2,1,0:T(8,128)(2,1)S(1)}, bf16[8,2,512,256]{3,2,1,0:T(8,128)(2,1)}, u32[]{:S(2)}) copy-start(bf16[8,2,512,256]{3,2,1,0:T(8,128)(2,1)} %value_ref.3) | copy-start | bytes 12582916
  0.6 3.5 %copy-start = (bf16[8,2,512,256]{3,2,1,0:T(8,128)(2,1)S(1)}, bf16[8,2,512,256]{3,2,1,0:T(8,128)(2,1)}, u32[]{:S(2)}) copy-start(bf16[8,2,512,256]{3,2,1,0:T(8,128)(2,1)} %key_ref.3) | copy-start | bytes 12582916
  7.6 12.6 %collective-permute-start.6 = (f32[4,8,2,8,128]{4,3,2,1,0:T(8,128)S(1)}, f32[4,8,2,8,128]{4,3,2,1,0:T(8,128)S(1)}, u32[]{:S(2)}, u32[]{:S(2)}) collective-permute-start(f32[4,8,2,8,128]{4,3,2,1,0:T(8,128)S(1)} %get-tuple-element.19), channel_id=1, source_target_pairs={{0,1},{1,0},{2,3},{3,2},{4,5},{5,4},{6,7},{7,6},{8,9},{9,8},{10,11... | collective-permute-start | bytes 786440 | tf_op jit(solution)/shard_map/ppermute | solution.py:159
  8.1 1.3 %collective-permute-start = (f32[8,16,128]{2,1,0:T(8,128)S(1)}, f32[8,16,128]{2,1,0:T(8,128)S(1)}, u32[]{:S(2)}, u32[]{:S(2)}) collective-permute-start(f32[8,16,128]{2,1,0:T(8,128)S(1)} %get-tuple-element.14), channel_id=1, source_target_pairs={{0,1},{1,0},{2,3},{3,2},{4,5},{5,4},{6,7},{7,6},{8,9},{9,8},{10,11... | collective-permute-start | bytes 196616 | tf_op jit(solution)/shard_map/ppermute | solution.py:159
  9.4 5.4 %collective-permute-start.1 = (f32[8,16,128]{2,1,0:T(8,128)S(1)}, f32[8,16,128]{2,1,0:T(8,128)S(1)}, u32[]{:S(2)}, u32[]{:S(2)}) collective-permute-start(f32[8,16,128]{2,1,0:T(8,128)S(1)} %add.36), channel_id=1, source_target_pairs={{0,2},{1,3},{2,0},{3,1},{4,6},{5,7},{6,4},{7,5},{8,10},{9,11},{10,... | collective-permute-start | bytes 196616 | tf_op jit(solution)/shard_map/ppermute | solution.py:159
  14.8 5.3 %collective-permute-start.2 = (f32[8,16,128]{2,1,0:T(8,128)S(1)}, f32[8,16,128]{2,1,0:T(8,128)S(1)}, u32[]{:S(2)}, u32[]{:S(2)}) collective-permute-start(f32[8,16,128]{2,1,0:T(8,128)S(1)} %add.37), channel_id=1, source_target_pairs={{0,4},{1,5},{2,6},{3,7},{4,0},{5,1},{6,2},{7,3},{8,12},{9,13},{10,... | collective-permute-start | bytes 196616 | tf_op jit(solution)/shard_map/ppermute | solution.py:159
  20.1 4.1 %collective-permute-start.3 = (f32[8,16,128]{2,1,0:T(8,128)S(1)}, f32[8,16,128]{2,1,0:T(8,128)S(1)}, u32[]{:S(2)}, u32[]{:S(2)}) collective-permute-start(f32[8,16,128]{2,1,0:T(8,128)S(1)} %add.38), channel_id=1, source_target_pairs={{0,9},{1,8},{2,11},{3,10},{4,13},{5,12},{6,15},{7,14},{8,1},{9,0},... | collective-permute-start | bytes 196616 | tf_op jit(solution)/shard_map/ppermute | solution.py:159
  20.2 7.5 %collective-permute-start.8 = (f32[8,2,8,128]{3,2,1,0:T(8,128)S(1)}, f32[8,2,8,128]{3,2,1,0:T(8,128)S(1)}, u32[]{:S(2)}, u32[]{:S(2)}) collective-permute-start(f32[8,2,8,128]{3,2,1,0:T(8,128)S(1)} %get-tuple-element.22), channel_id=1, source_target_pairs={{0,2},{1,3},{2,0},{3,1},{4,6},{5,7},{6,4},{7,5},{8,10},{9,11},{10,... | collective-permute-start | bytes 196616 | tf_op jit(solution)/shard_map/ppermute | solution.py:159
  24.2 6.7 %collective-permute-start.4 = (f32[8,16,128]{2,1,0:T(8,128)S(1)}, f32[8,16,128]{2,1,0:T(8,128)S(1)}, u32[]{:S(2)}, u32[]{:S(2)}) collective-permute-start(f32[8,16,128]{2,1,0:T(8,128)S(1)} %add.39), channel_id=1, source_target_pairs={{0,17},{1,16},{2,19},{3,18},{4,21},{5,20},{6,23},{7,22},{8,25},{9,... | collective-permute-start | bytes 196616 | tf_op jit(solution)/shard_map/ppermute | solution.py:159
  26.1 5.2 %collective-permute-start.7 = (f32[8,2,8,128]{3,2,1,0:T(8,128)S(1)}, f32[8,2,8,128]{3,2,1,0:T(8,128)S(1)}, u32[]{:S(2)}, u32[]{:S(2)}) collective-permute-start(f32[8,2,8,128]{3,2,1,0:T(8,128)S(1)} %get-tuple-element.23), channel_id=1, source_target_pairs={{0,2},{1,3},{2,0},{3,1},{4,6},{5,7},{6,4},{7,5},{8,10},{9,11},{10,... | collective-permute-start | bytes 196616 | tf_op jit(solution)/shard_map/ppermute | solution.py:159
  27.7 7.0 %collective-permute-start.9 = (f32[8,2,8,128]{3,2,1,0:T(8,128)S(1)}, f32[8,2,8,128]{3,2,1,0:T(8,128)S(1)}, u32[]{:S(2)}, u32[]{:S(2)}) collective-permute-start(f32[8,2,8,128]{3,2,1,0:T(8,128)S(1)} %fusion.2), channel_id=1, source_target_pairs={{0,4},{1,5},{2,6},{3,7},{4,0},{5,1},{6,2},{7,3},{8,12},{9,13},{10,... | collective-permute-start | bytes 196616 | tf_op jit(solution)/shard_map/ppermute | solution.py:159
  31.2 1.2 %collective-permute-start.5 = (f32[8,128]{1,0:T(8,128)S(1)}, f32[8,128]{1,0:T(8,128)S(1)}, u32[]{:S(2)}, u32[]{:S(2)}) collective-permute-start(f32[8,128]{1,0:T(8,128)S(1)} %threshold.1.own_ref), channel_id=1, source_target_pairs={{0,1},{1,0},{2,3},{3,2},{4,5},{5,4},{6,7},{7,6},{8,9},{9,8},{10,11... | collective-permute-start | bytes 12296 | tf_op jit(solution)/shard_map/ppermute | solution.py:159
where the time goes:
time: 35.5 us; the launch traced here: 35.4 us
  starting transfers between devices  15.4 us (43%)
  waiting for transfers between devices  11.4 us (32%)
  Pallas kernels  6.1 us (17%)
  local copies, waits for them, and re-layouts  1.7 us (5%)
  between operations  0.73 us (2%)
    ppermute x10, starting transfers between devices, permute(): return lax.ppermute(x, ('tensor', 'seq'), pairing)  15.4 us
    ppermute x10, waiting for transfers between devices, permute(): return lax.ppermute(x, ('tensor', 'seq'), pairing)  11.4 us
    pallas_call x2, Pallas kernels, per_device(): pl.pallas_call(functools.partial(hist_kernel, ranges, range(pairs)[SPLIT[...  3.45 us
    pallas_call x1, Pallas kernels, per_device(): pl.pallas_call(count_kernel, out_shape=(half, half, jax.ShapeDtypeStruct(...  1.76 us
    unnamed x4, local copies, waits for them, and re-layouts  1.7 us
  transfers between devices with their start and end apart: 10, of which 6 were waited for; matrix products, arithmetic and copies ran while one was open for 0% of the time, Pallas kernels for 1%

commit v1 on v0

--- a/solution.py
+++ b/solution.py
@@ -67,7 +67,7 @@
     half = ranges // 2
     away = (block >= half).astype(jnp.int32)
     block = block - half * away
-    block = 2 * block + away
+    block = 2 * block + (parity(block, half) ^ away)
     high = (block ^ lax.axis_index("seq")) * per + index % per
     is_key = (index // per) % 2 == 0
     for p in work:
@@ -192,10 +192,7 @@
     while bit < ranges:
         mine = plus(mine, permute(mine, 0, bit))
         bit *= 2
-    bit = 1
-    while bit < columns:
-        mine = plus(mine, permute(mine, bit, 1))
-        bit *= 2
+    mine = functools.reduce(jnp.add, [mine] + [permute(mine, k, k.bit_count() & 1) for k in range(1, columns)])
     everything = float(tokens * ranges * heads * lax.axis_size("tensor"))
     found = pl.pallas_call(
         functools.partial(threshold_kernel, everything),
@@ -214,7 +211,7 @@
     while bit < ranges:
         kept = []
         for j in range(0, len(parts), 2):
-            part = permute(total(parts[j + 1]), 0, bit)
+            part = permute(total(parts[j + 1]), 0, bit | 1)
             kept.append([*parts[j], part])
         parts = kept
         bit *= 2

time: 35.5 us -> 32.9 us (0.927)
  waiting for transfers between devices: 11.4 us -> 9.28 us
  starting transfers between devices: 15.4 us -> 14.8 us
    ppermute x10 -> x11, waiting for transfers between devices: 11.4 us -> 9.28 us  [permute(): return lax.ppermute(x, ('tensor', 'seq'), pairing)]
    ppermute x10 -> x11, starting transfers between devices: 15.4 us -> 14.8 us  [permute(): return lax.ppermute(x, ('tensor', 'seq'), pairing)]
  transfers between devices with their start and end apart: 10 -> 11, of which waited for: 6 -> 5; matrix products, arithmetic and copies ran while one was open for 0% -> 0% of each run, Pallas kernels for 1% -> 1%
where the time goes in v1:
time: 32.9 us; the launch traced here: 32.7 us
  starting transfers between devices  14.8 us (45%)
  waiting for transfers between devices  9.28 us (28%)
  Pallas kernels  6.1 us (19%)
  local copies, waits for them, and re-layouts  1.7 us (5%)
  between operations  0.71 us (2%)
    ppermute x11, starting transfers between devices, permute(): return lax.ppermute(x, ('tensor', 'seq'), pairing)  14.8 us
    ppermute x11, waiting for transfers between devices, permute(): return lax.ppermute(x, ('tensor', 'seq'), pairing)  9.28 us
    pallas_call x2, Pallas kernels, per_device(): pl.pallas_call(functools.partial(hist_kernel, ranges, range(pairs)[SPLIT[...  3.46 us
    pallas_call x1, Pallas kernels, per_device(): pl.pallas_call(count_kernel, out_shape=(half, half, jax.ShapeDtypeStruct(...  1.76 us
    unnamed x4, local copies, waits for them, and re-layouts  1.7 us
    pallas_call x1, Pallas kernels, per_device(): pl.pallas_call(final_kernel, out_shape=(jax.ShapeDtypeStruct((pairs, head...  0.67 us
  transfers between devices with their start and end apart: 11, of which 5 were waited for; matrix products, arithmetic and copies ran while one was open for 0% of the time, Pallas kernels for 1%

profile of v1, /device:TPU:0, one launch (start us, length us, event | category | flops | bytes accessed | tf_op | source)
XLA Modules:
  0.0 32.7 jit_solution(18341638988803800248)
XLA Ops:
  0.6 0.0 copy-start.1
  0.6 0.0 copy-start
  0.7 1.8 %counts.1 = (f32[8,16,128]{2,1,0:T(8,128)S(1)}, f32[8,16,128]{2,1,0:T(8,128)S(1)}, s32[8,2,512]{2,1,0:T(2,128)S(1)}, f32[8,128]{1,0:T(8,128)S(1)}) custom-call(s32[8,2,512]{2,1,0:T(2,128)} %bin_ref.1, s32[8]{0:T(128)} %target_ref.1), custom_call_target="tpu_custom_call" | custom-call | flops 10000000000 | bytes 100000000 | tf_op jit(solution)/shard_map/counts/pallas_call | solution.py:164
  2.4 0.4 %copy-done.1 = bf16[8,2,512,256]{3,2,1,0:T(8,128)(2,1)S(1)} copy-done((bf16[8,2,512,256]{3,2,1,0:T(8,128)(2,1)S(1)}, bf16[8,2,512,256]{3,2,1,0:T(8,128)(2,1)}, u32[]{:S(2)}) %copy-start.1) | copy-done | bytes 4194328
  2.8 1.3 %copy-done = bf16[8,2,512,256]{3,2,1,0:T(8,128)(2,1)S(1)} copy-done((bf16[8,2,512,256]{3,2,1,0:T(8,128)(2,1)S(1)}, bf16[8,2,512,256]{3,2,1,0:T(8,128)(2,1)}, u32[]{:S(2)}) %copy-start) | copy-done | bytes 4194328
  4.1 2.1 %hist.2 = (f32[4,8,2,8,128]{4,3,2,1,0:T(8,128)S(1)}, f32[4,8,2,8,128]{4,3,2,1,0:T(8,128)S(1)}) custom-call(bf16[8,2,512,256]{3,2,1,0:T(8,128)(2,1)S(1)} %copy-done, bf16[8,2,512,256]{3,2,1,0:T(8,128)(2,1)S(1)} %copy-done.1, s32[8,2,512]{2,1,0:T(2,128)S(1)} %get-tuple-element.15.bins), custom_call_target="tpu_custom_call" | custom-call | tf_op jit(solution)/shard_map/hist/pallas_call | solution.py:176
  6.2 1.4 %hist.3 = (f32[4,8,2,8,128]{4,3,2,1,0:T(8,128)S(1)}, f32[4,8,2,8,128]{4,3,2,1,0:T(8,128)S(1)}) custom-call(bf16[8,2,512,256]{3,2,1,0:T(8,128)(2,1)S(1)} %copy-done, bf16[8,2,512,256]{3,2,1,0:T(8,128)(2,1)S(1)} %copy-done.1, s32[8,2,512]{2,1,0:T(2,128)S(1)} %get-tuple-element.15.bins, ...), custom_call_target="tpu_custom_call", output_to_operand_aliasing={{0}: (3, {}), {1}: (4, {})} | custom-call | tf_op jit(solution)/shard_map/hist/pallas_call | solution.py:176
  7.6 0.6 %collective-permute-start.7 = (f32[4,8,2,8,128]{4,3,2,1,0:T(8,128)S(1)}, f32[4,8,2,8,128]{4,3,2,1,0:T(8,128)S(1)}, u32[]{:S(2)}, u32[]{:S(2)}) collective-permute-start(f32[4,8,2,8,128]{4,3,2,1,0:T(8,128)S(1)} %get-tuple-element.19), channel_id=1, source_target_pairs={{0,1},{1,0},{2,3},{3,2},{4,5},{5,4},{6,7},{7,6},{8,9},{9,8},{10,11... | collective-permute-start | bytes 786440 | tf_op jit(solution)/shard_map/ppermute | solution.py:159
  8.1 0.1 collective-permute-start
  8.2 1.2 %collective-permute-done = f32[8,16,128]{2,1,0:T(8,128)S(1)} collective-permute-done((f32[8,16,128]{2,1,0:T(8,128)S(1)}, f32[8,16,128]{2,1,0:T(8,128)S(1)}, u32[]{:S(2)}, u32[]{:S(2)}) %collective-permute-start) | collective-permute-done | bytes 65568 | tf_op jit(solution)/shard_map/ppermute | solution.py:159
  9.4 3.0 %collective-permute-start.1 = (f32[8,16,128]{2,1,0:T(8,128)S(1)}, f32[8,16,128]{2,1,0:T(8,128)S(1)}, u32[]{:S(2)}, u32[]{:S(2)}) collective-permute-start(f32[8,16,128]{2,1,0:T(8,128)S(1)} %add.39), channel_id=1, source_target_pairs={{0,2},{1,3},{2,0},{3,1},{4,6},{5,7},{6,4},{7,5},{8,10},{9,11},{10,... | collective-permute-start | bytes 196616 | tf_op jit(solution)/shard_map/ppermute | solution.py:159
  12.4 2.4 %collective-permute-done.1 = f32[8,16,128]{2,1,0:T(8,128)S(1)} collective-permute-done((f32[8,16,128]{2,1,0:T(8,128)S(1)}, f32[8,16,128]{2,1,0:T(8,128)S(1)}, u32[]{:S(2)}, u32[]{:S(2)}) %collective-permute-start.1) | collective-permute-done | bytes 65568 | tf_op jit(solution)/shard_map/ppermute | solution.py:159
  14.8 3.0 %collective-permute-start.2 = (f32[8,16,128]{2,1,0:T(8,128)S(1)}, f32[8,16,128]{2,1,0:T(8,128)S(1)}, u32[]{:S(2)}, u32[]{:S(2)}) collective-permute-start(f32[8,16,128]{2,1,0:T(8,128)S(1)} %add.40), channel_id=1, source_target_pairs={{0,4},{1,5},{2,6},{3,7},{4,0},{5,1},{6,2},{7,3},{8,12},{9,13},{10,... | collective-permute-start | bytes 196616 | tf_op jit(solution)/shard_map/ppermute | solution.py:159
  17.8 0.0 collective-permute-done.7
  17.8 0.1 collective-permute-start.9
  17.9 2.2 %collective-permute-done.2 = f32[8,16,128]{2,1,0:T(8,128)S(1)} collective-permute-done((f32[8,16,128]{2,1,0:T(8,128)S(1)}, f32[8,16,128]{2,1,0:T(8,128)S(1)}, u32[]{:S(2)}, u32[]{:S(2)}) %collective-permute-start.2) | collective-permute-done | bytes 65568 | tf_op jit(solution)/shard_map/ppermute | solution.py:159
  20.1 2.8 %collective-permute-start.5 = (f32[8,16,128]{2,1,0:T(8,128)S(1)}, f32[8,16,128]{2,1,0:T(8,128)S(1)}, u32[]{:S(2)}, u32[]{:S(2)}) collective-permute-start(f32[8,16,128]{2,1,0:T(8,128)S(1)} %add.41), channel_id=1, source_target_pairs={{0,24},{1,25},{2,26},{3,27},{4,28},{5,29},{6,30},{7,31},{8,16},{9,... | collective-permute-start | bytes 196616 | tf_op jit(solution)/shard_map/ppermute | solution.py:159
  22.9 0.0 collective-permute-start.4
  22.9 0.5 %collective-permute-start.3 = (f32[8,16,128]{2,1,0:T(8,128)S(1)}, f32[8,16,128]{2,1,0:T(8,128)S(1)}, u32[]{:S(2)}, u32[]{:S(2)}) collective-permute-start(f32[8,16,128]{2,1,0:T(8,128)S(1)} %add.41), channel_id=1, source_target_pairs={{0,9},{1,8},{2,11},{3,10},{4,13},{5,12},{6,15},{7,14},{8,1},{9,0},... | collective-permute-start | bytes 196616 | tf_op jit(solution)/shard_map/ppermute | solution.py:159
  23.4 2.0 %collective-permute-start.8 = (f32[8,2,8,128]{3,2,1,0:T(8,128)S(1)}, f32[8,2,8,128]{3,2,1,0:T(8,128)S(1)}, u32[]{:S(2)}, u32[]{:S(2)}) collective-permute-start(f32[8,2,8,128]{3,2,1,0:T(8,128)S(1)} %get-tuple-element.23), channel_id=1, source_target_pairs={{0,3},{1,2},{2,1},{3,0},{4,7},{5,6},{6,5},{7,4},{8,11},{9,10},{10,... | collective-permute-start | bytes 196616 | tf_op jit(solution)/shard_map/ppermute | solution.py:159
  25.4 0.0 collective-permute-done.9
  25.4 2.8 %collective-permute-start.10 = (f32[8,2,8,128]{3,2,1,0:T(8,128)S(1)}, f32[8,2,8,128]{3,2,1,0:T(8,128)S(1)}, u32[]{:S(2)}, u32[]{:S(2)}) collective-permute-start(f32[8,2,8,128]{3,2,1,0:T(8,128)S(1)} %fusion.2), channel_id=1, source_target_pairs={{0,5},{1,4},{2,7},{3,6},{4,1},{5,0},{6,3},{7,2},{8,13},{9,12},{10,... | collective-permute-start | bytes 196616 | tf_op jit(solution)/shard_map/ppermute | solution.py:159
  28.2 0.0 collective-permute-done.5
  28.2 0.0 collective-permute-done.4
  28.2 0.0 collective-permute-done.3
  28.2 0.2 threshold.1.own_ref
  28.4 0.1 collective-permute-start.6
  28.5 1.2 %collective-permute-done.6.other_ref = f32[8,128]{1,0:T(8,128)S(1)} collective-permute-done((f32[8,128]{1,0:T(8,128)S(1)}, f32[8,128]{1,0:T(8,128)S(1)}, u32[]{:S(2)}, u32[]{:S(2)}) %collective-permute-start.6) | collective-permute-done | bytes 4128 | tf_op jit(solution)/shard_map/ppermute | solution.py:159
  29.7 0.0 collective-permute-done.8.refs_2_
  29.7 2.3 %collective-permute-done.10.refs_3_ = f32[8,2,8,128]{3,2,1,0:T(8,128)S(1)} collective-permute-done((f32[8,2,8,128]{3,2,1,0:T(8,128)S(1)}, f32[8,2,8,128]{3,2,1,0:T(8,128)S(1)}, u32[]{:S(2)}, u32[]{:S(2)}) %collective-permute-start.10) | collective-permute-done | bytes 65568 | tf_op jit(solution)/shard_map/ppermute | solution.py:159
  32.0 0.7 %final.1 = (f32[8,2,2,512]{3,2,1,0:T(2,128)}, s32[1,8]{1,0:T(1,128)}) custom-call(f32[8,128]{1,0:T(8,128)S(1)} %threshold.1.own_ref, f32[8,128]{1,0:T(8,128)S(1)} %collective-permute-done.6.other_ref, f32[8,2,8,128]{3,2,1,0:T(8,128)S(1)} %get-tuple-element.24.refs_0_, f32[8,2,8,128]{3,2,1,0:T(8,128)S(1)} %get-tuple-element.25.refs_1_, ...), custom_call_target="tpu_custom_call" | custom-call | tf_op jit(solution)/shard_map/final/pallas_call | solution.py:219
  (6 shorter events, 0.1 us)
Async XLA Ops:
  0.6 2.2 %copy-start.1 = (bf16[8,2,512,256]{3,2,1,0:T(8,128)(2,1)S(1)}, bf16[8,2,512,256]{3,2,1,0:T(8,128)(2,1)}, u32[]{:S(2)}) copy-start(bf16[8,2,512,256]{3,2,1,0:T(8,128)(2,1)} %value_ref.3) | copy-start | bytes 12582916
  0.6 3.5 %copy-start = (bf16[8,2,512,256]{3,2,1,0:T(8,128)(2,1)S(1)}, bf16[8,2,512,256]{3,2,1,0:T(8,128)(2,1)}, u32[]{:S(2)}) copy-start(bf16[8,2,512,256]{3,2,1,0:T(8,128)(2,1)} %key_ref.3) | copy-start | bytes 12582916
  7.6 10.2 %collective-permute-start.7 = (f32[4,8,2,8,128]{4,3,2,1,0:T(8,128)S(1)}, f32[4,8,2,8,128]{4,3,2,1,0:T(8,128)S(1)}, u32[]{:S(2)}, u32[]{:S(2)}) collective-permute-start(f32[4,8,2,8,128]{4,3,2,1,0:T(8,128)S(1)} %get-tuple-element.19), channel_id=1, source_target_pairs={{0,1},{1,0},{2,3},{3,2},{4,5},{5,4},{6,7},{7,6},{8,9},{9,8},{10,11... | collective-permute-start | bytes 786440 | tf_op jit(solution)/shard_map/ppermute | solution.py:159
  8.1 1.3 %collective-permute-start = (f32[8,16,128]{2,1,0:T(8,128)S(1)}, f32[8,16,128]{2,1,0:T(8,128)S(1)}, u32[]{:S(2)}, u32[]{:S(2)}) collective-permute-start(f32[8,16,128]{2,1,0:T(8,128)S(1)} %get-tuple-element.14), channel_id=1, source_target_pairs={{0,1},{1,0},{2,3},{3,2},{4,5},{5,4},{6,7},{7,6},{8,9},{9,8},{10,11... | collective-permute-start | bytes 196616 | tf_op jit(solution)/shard_map/ppermute | solution.py:159
  9.4 5.4 %collective-permute-start.1 = (f32[8,16,128]{2,1,0:T(8,128)S(1)}, f32[8,16,128]{2,1,0:T(8,128)S(1)}, u32[]{:S(2)}, u32[]{:S(2)}) collective-permute-start(f32[8,16,128]{2,1,0:T(8,128)S(1)} %add.39), channel_id=1, source_target_pairs={{0,2},{1,3},{2,0},{3,1},{4,6},{5,7},{6,4},{7,5},{8,10},{9,11},{10,... | collective-permute-start | bytes 196616 | tf_op jit(solution)/shard_map/ppermute | solution.py:159
  14.8 5.3 %collective-permute-start.2 = (f32[8,16,128]{2,1,0:T(8,128)S(1)}, f32[8,16,128]{2,1,0:T(8,128)S(1)}, u32[]{:S(2)}, u32[]{:S(2)}) collective-permute-start(f32[8,16,128]{2,1,0:T(8,128)S(1)} %add.40), channel_id=1, source_target_pairs={{0,4},{1,5},{2,6},{3,7},{4,0},{5,1},{6,2},{7,3},{8,12},{9,13},{10,... | collective-permute-start | bytes 196616 | tf_op jit(solution)/shard_map/ppermute | solution.py:159
  17.8 7.6 %collective-permute-start.9 = (f32[8,2,8,128]{3,2,1,0:T(8,128)S(1)}, f32[8,2,8,128]{3,2,1,0:T(8,128)S(1)}, u32[]{:S(2)}, u32[]{:S(2)}) collective-permute-start(f32[8,2,8,128]{3,2,1,0:T(8,128)S(1)} %get-tuple-element.22), channel_id=1, source_target_pairs={{0,3},{1,2},{2,1},{3,0},{4,7},{5,6},{6,5},{7,4},{8,11},{9,10},{10,... | collective-permute-start | bytes 196616 | tf_op jit(solution)/shard_map/ppermute | solution.py:159
  20.1 8.1 %collective-permute-start.5 = (f32[8,16,128]{2,1,0:T(8,128)S(1)}, f32[8,16,128]{2,1,0:T(8,128)S(1)}, u32[]{:S(2)}, u32[]{:S(2)}) collective-permute-start(f32[8,16,128]{2,1,0:T(8,128)S(1)} %add.41), channel_id=1, source_target_pairs={{0,24},{1,25},{2,26},{3,27},{4,28},{5,29},{6,30},{7,31},{8,16},{9,... | collective-permute-start | bytes 196616 | tf_op jit(solution)/shard_map/ppermute | solution.py:159
  22.9 5.3 %collective-permute-start.4 = (f32[8,16,128]{2,1,0:T(8,128)S(1)}, f32[8,16,128]{2,1,0:T(8,128)S(1)}, u32[]{:S(2)}, u32[]{:S(2)}) collective-permute-start(f32[8,16,128]{2,1,0:T(8,128)S(1)} %add.41), channel_id=1, source_target_pairs={{0,17},{1,16},{2,19},{3,18},{4,21},{5,20},{6,23},{7,22},{8,25},{9,... | collective-permute-start | bytes 196616 | tf_op jit(solution)/shard_map/ppermute | solution.py:159
  22.9 5.3 %collective-permute-start.3 = (f32[8,16,128]{2,1,0:T(8,128)S(1)}, f32[8,16,128]{2,1,0:T(8,128)S(1)}, u32[]{:S(2)}, u32[]{:S(2)}) collective-permute-start(f32[8,16,128]{2,1,0:T(8,128)S(1)} %add.41), channel_id=1, source_target_pairs={{0,9},{1,8},{2,11},{3,10},{4,13},{5,12},{6,15},{7,14},{8,1},{9,0},... | collective-permute-start | bytes 196616 | tf_op jit(solution)/shard_map/ppermute | solution.py:159
  23.4 6.3 %collective-permute-start.8 = (f32[8,2,8,128]{3,2,1,0:T(8,128)S(1)}, f32[8,2,8,128]{3,2,1,0:T(8,128)S(1)}, u32[]{:S(2)}, u32[]{:S(2)}) collective-permute-start(f32[8,2,8,128]{3,2,1,0:T(8,128)S(1)} %get-tuple-element.23), channel_id=1, source_target_pairs={{0,3},{1,2},{2,1},{3,0},{4,7},{5,6},{6,5},{7,4},{8,11},{9,10},{10,... | collective-permute-start | bytes 196616 | tf_op jit(solution)/shard_map/ppermute | solution.py:159
  25.4 6.6 %collective-permute-start.10 = (f32[8,2,8,128]{3,2,1,0:T(8,128)S(1)}, f32[8,2,8,128]{3,2,1,0:T(8,128)S(1)}, u32[]{:S(2)}, u32[]{:S(2)}) collective-permute-start(f32[8,2,8,128]{3,2,1,0:T(8,128)S(1)} %fusion.2), channel_id=1, source_target_pairs={{0,5},{1,4},{2,7},{3,6},{4,1},{5,0},{6,3},{7,2},{8,13},{9,12},{10,... | collective-permute-start | bytes 196616 | tf_op jit(solution)/shard_map/ppermute | solution.py:159
  28.4 1.2 %collective-permute-start.6 = (f32[8,128]{1,0:T(8,128)S(1)}, f32[8,128]{1,0:T(8,128)S(1)}, u32[]{:S(2)}, u32[]{:S(2)}) collective-permute-start(f32[8,128]{1,0:T(8,128)S(1)} %threshold.1.own_ref), channel_id=1, source_target_pairs={{0,1},{1,0},{2,3},{3,2},{4,5},{5,4},{6,7},{7,6},{8,9},{9,8},{10,11... | collective-permute-start | bytes 12296 | tf_op jit(solution)/shard_map/ppermute | solution.py:159
